TPU v7x, 512 devices: a whole 4x4x16 slice. The times are simulated.
512 devices in a mesh: nodes: 128 (over z_hi, y, x, core), heads: 4 (over z_lo).
Axes of the slice: x: 4, y: 4, z: 16 (z_hi: 4, z_lo: 4; z = z_hi * 4 + z_lo), core: 2. Of those that a mesh axis runs over, the one named last changes fastest.
Arguments:
- grid_state: bfloat16 [131072, 1024], P('nodes', 'heads'), may hold values from -6 to 6
- mesh_state: bfloat16 [32768, 1024], P('nodes', 'heads'), may hold values from -6 to 6
- encoder_query: bfloat16 [1024, 512], P('nodes', 'heads'), may hold values from -0.1875 to 0.1875
- encoder_key: bfloat16 [1024, 512], P('nodes', 'heads'), may hold values from -0.1875 to 0.1875
- encoder_value: bfloat16 [1024, 512], P('nodes', 'heads'), may hold values from -0.1875 to 0.1875
- encoder_output: bfloat16 [512, 1024], P('heads', 'nodes'), may hold values from -0.25 to 0.25
- window_query: bfloat16 [1024, 512], P('nodes', 'heads'), may hold values from -0.1875 to 0.1875
- window_key: bfloat16 [1024, 512], P('nodes', 'heads'), may hold values from -0.1875 to 0.1875
- window_value: bfloat16 [1024, 512], P('nodes', 'heads'), may hold values from -0.1875 to 0.1875
- window_output: bfloat16 [512, 1024], P('heads', 'nodes'), may hold values from -0.25 to 0.25
- expand_weight: bfloat16 [1024, 2048], P('nodes', 'heads'), may hold values from -0.1875 to 0.1875
- shrink_weight: bfloat16 [2048, 1024], P('heads', 'nodes'), may hold values from -0.125 to 0.125
- decoder_query: bfloat16 [1024, 512], P('nodes', 'heads'), may hold values from -0.1875 to 0.1875
- decoder_key: bfloat16 [1024, 512], P('nodes', 'heads'), may hold values from -0.1875 to 0.1875
- decoder_value: bfloat16 [1024, 512], P('nodes', 'heads'), may hold values from -0.1875 to 0.1875
- decoder_output: bfloat16 [512, 1024], P('heads', 'nodes'), may hold values from -0.25 to 0.25
- encoder_blocks: int32 [256, 8], P('nodes'), may hold values from 0 to 1023, as said below
- encoder_count: int32 [256], P('nodes'), may hold values from 2 to 8, as said below
- window_offsets: int32 [256, 4], P('nodes'), may hold values from -2 to 2, as said below
- decoder_blocks: int32 [1024, 3], P('nodes'), may hold values from 0 to 255, as said below
- decoder_count: int32 [1024], P('nodes'), may hold values from 1 to 3, as said below
Outputs:
- grid_out: bfloat16 [131072, 1024], P('nodes', 'heads')
- mesh_out: bfloat16 [32768, 1024], P('nodes', 'heads')
Inputs may be any that keep to these rules, and one draw needn't show every extreme that they name: `encoder_blocks`: row m names 8 different grid blocks; each lies among the grid blocks of the index of nodes that holds mesh block m, or in the nearer half of the grid blocks of the index on either side. The first encoder_count[m] slots of row m are live; every mesh block held by the first or last eighth of the indices of nodes has all 8 slots live. `window_offsets`: each row holds 4 different offsets, the first of them 0. `decoder_blocks`: row g names 3 different mesh blocks; each lies among the mesh blocks of the index of nodes that holds grid block g, or is the one block next to them on either side. The first decoder_count[g] slots of row g are live; every grid block of the first index of nodes has all 3 slots live.
All inputs are finite; a program needn't handle non-finite values.
Results may differ from a plain program's by a relative error of at most 0.012.
Values may be sent and summed in bfloat16 or wider, within the bound.
No kernel may reach another device: no remote copies, remote signals or barrier semaphores. Data moves between devices by JAX's collectives and lax.ppermute only.
A program may use at most 64 MiB of HBM per device.

v0:
```python
import math
import jax
import jax.numpy as jnp
from jax import lax
from jax.sharding import PartitionSpec as P

HEAD_DIM = 64
TILE = 128
EPSILON = 1e-05


def turned_gather(arrays, axis, dims):
    turned = [jnp.moveaxis(a, dim, 0) for a, dim in zip(arrays, dims)]
    widths = [t[0].size for t in turned]
    both = jnp.concatenate([t.reshape(-1, w) for t, w in zip(turned, widths)], axis=1)
    whole = lax.all_gather(both, axis, axis=0, tiled=True)
    parts = jnp.split(whole, [sum(widths[:k]) for k in range(1, len(widths))], axis=1)
    return tuple(
        (
            jnp.moveaxis(b.reshape(-1, *t.shape[1:]), 0, dim)
            for b, t, dim in zip(parts, turned, dims)
        )
    )


def in_order(parts, dim):
    lengths = list(parts.shape[1:])
    lengths[dim] *= parts.shape[0]
    return jnp.moveaxis(parts, 0, dim).reshape(lengths)


def from_everyone(x, axis):
    length = lax.axis_size(axis)
    return lax.all_to_all(jnp.broadcast_to(x[None], (length, *x.shape)), axis, 0, 0, tiled=True)


def collect(x, axis, dim):
    return in_order(from_everyone(x, axis), dim)


def with_halo(x, sides, width):
    for axis, dim in sides:
        size, length = (lax.axis_size(axis), x.shape[dim])
        up = [(i, (i + 1) % size) for i in range(size - 1)]
        down = [(j, i) for i, j in up]
        last = lax.slice_in_dim(x, length - width, length, axis=dim)
        first = lax.slice_in_dim(x, 0, width, axis=dim)
        before = lax.ppermute(last, axis, up)
        after = lax.ppermute(first, axis, down)
        x = jnp.concatenate([before, x, after], axis=dim)
    return x


def in_blocks(x, dim, length):
    before, after = (x.shape[:dim], x.shape[dim + 1 :])
    return jnp.moveaxis(x.reshape(*before, length, -1, *after), dim, 0)


def sum_at_owner(x, axis, dim):
    parts = in_blocks(x, dim, lax.axis_size(axis))
    arrived = lax.all_to_all(parts, axis, split_axis=0, concat_axis=0, tiled=True)
    return arrived.astype(jnp.float32).sum(axis=0)


def normalize(values):
    values = values.astype(jnp.float32)
    average = jnp.mean(values, axis=-1, keepdims=True)
    centred = values - average
    spread = jnp.mean(centred * centred, axis=-1, keepdims=True)
    return (centred * lax.rsqrt(spread + EPSILON)).astype(jnp.bfloat16)


def local_terms(source, weight_list):
    return tuple(
        (jnp.dot(source, member, preferred_element_type=jnp.float32) for member in weight_list)
    )


def fold_parts(pieces, row_count):
    group_count = pieces.shape[0] // row_count
    return jnp.sum(pieces.reshape(group_count, row_count, pieces.shape[1]), axis=0)


def attend(queries, key_rows, value_rows, key_mask):
    batch_size, row_count, column_count = queries.shape
    head_count = column_count // HEAD_DIM
    split_query = queries.reshape(batch_size, row_count, head_count, HEAD_DIM)
    split_key = key_rows.reshape(batch_size, key_rows.shape[1], head_count, HEAD_DIM)
    split_value = value_rows.reshape(batch_size, value_rows.shape[1], head_count, HEAD_DIM)
    scores = jnp.einsum(
        "bqhd,bkhd->bhqk", split_query, split_key, preferred_element_type=jnp.float32
    )
    scores = jnp.where(key_mask[:, None, None, :], scores, -1e30)
    highest = jnp.max(scores, axis=-1, keepdims=True)
    weights = jnp.exp(scores - highest)
    weights = (weights / jnp.sum(weights, axis=-1, keepdims=True)).astype(jnp.bfloat16)
    mixture = jnp.einsum(
        "bhqk,bkhd->bqhd", weights, split_value, preferred_element_type=jnp.float32
    )
    return mixture.reshape(batch_size, row_count, column_count).astype(jnp.bfloat16)


def attend_blocks(queries, key_rows, value_rows, key_mask):
    tile_count = queries.shape[0]
    group_size = math.gcd(tile_count, 4)

    def one_group(arguments):
        return attend(arguments[0], arguments[1], arguments[2], arguments[3])

    grouped = tuple(
        (
            member.reshape((tile_count // group_size, group_size) + member.shape[1:])
            for member in (queries, key_rows, value_rows, key_mask)
        )
    )
    return lax.map(one_group, grouped).reshape(queries.shape)


def pick_tiles(stacked, tile_count, chosen):
    column_count = stacked.shape[-1]
    tile_view = stacked.reshape(2, tile_count, TILE, column_count)
    picked = jnp.take(tile_view, chosen, axis=1)
    shaped = picked.reshape(2, chosen.shape[0], chosen.shape[1] * TILE, column_count)
    return (shaped[0], shaped[1])


def slot_mask(live_count, slot_total):
    live = jnp.arange(slot_total, dtype=jnp.int32)[None, :] < live_count[:, None]
    return jnp.repeat(live, TILE, axis=1)


def local(
    grid_state,
    mesh_state,
    encoder_query,
    encoder_key,
    encoder_value,
    encoder_output,
    window_query,
    window_key,
    window_value,
    window_output,
    expand_weight,
    shrink_weight,
    decoder_query,
    decoder_key,
    decoder_value,
    decoder_output,
    encoder_blocks,
    encoder_count,
    window_offsets,
    decoder_blocks,
    decoder_count,
):
    scaling = HEAD_DIM ** (-0.5)
    position = lax.axis_index("nodes")
    grid_rows = grid_state.shape[0]
    mesh_rows = mesh_state.shape[0]
    grid_tiles = grid_rows // TILE
    mesh_tiles = mesh_rows // TILE
    all_mesh_tiles = mesh_tiles * lax.axis_size("nodes")
    head_columns = encoder_key.shape[1]
    gathered = turned_gather(
        (
            encoder_query,
            encoder_key,
            encoder_value,
            encoder_output,
            window_query,
            window_key,
            window_value,
            window_output,
            expand_weight,
            shrink_weight,
            decoder_query,
            decoder_key,
            decoder_value,
            decoder_output,
        ),
        "nodes",
        (0, 0, 0, 1, 0, 0, 0, 1, 0, 1, 0, 0, 0, 1),
    )
    grid_full = collect(grid_state, "heads", 1)
    grid_norm = normalize(grid_full)
    grid_key, grid_value, grid_query = local_terms(
        grid_norm, (gathered[1], gathered[2], gathered[10])
    )
    grid_queries = (grid_query * scaling).astype(jnp.bfloat16)
    mesh_full = collect(mesh_state, "heads", 1)
    mesh_norm = normalize(mesh_full)
    (mesh_query,) = local_terms(mesh_norm, (gathered[0],))
    mesh_queries = (mesh_query * scaling).astype(jnp.bfloat16)
    rim_tiles = grid_tiles // 2
    stacked = jnp.stack([grid_key.astype(jnp.bfloat16), grid_value.astype(jnp.bfloat16)])
    padded = with_halo(stacked, (("nodes", 1),), rim_tiles * TILE)
    local_index = encoder_blocks - (position * grid_tiles - rim_tiles)
    key_rows, value_rows = pick_tiles(padded, grid_tiles + 2 * rim_tiles, local_index)
    key_mask = slot_mask(encoder_count, encoder_blocks.shape[1])
    encoded = attend_blocks(
        mesh_queries.reshape(mesh_tiles, TILE, head_columns), key_rows, value_rows, key_mask
    ).reshape(mesh_rows, head_columns)
    (encoder_terms,) = local_terms(encoded, (gathered[3],))
    encoder_pieces = lax.all_to_all(
        encoder_terms.astype(jnp.bfloat16), "heads", split_axis=1, concat_axis=0, tiled=True
    ).astype(encoder_terms.dtype)
    share_one = (mesh_state.astype(jnp.float32) + fold_parts(encoder_pieces, mesh_rows)).astype(
        jnp.bfloat16
    )
    mesh_one = collect(share_one, "heads", 1)
    norm_one = normalize(mesh_one)
    window_queries, window_keys, window_values = local_terms(
        norm_one, (gathered[4], gathered[5], gathered[6])
    )
    window_queries = (window_queries * scaling).astype(jnp.bfloat16)
    stacked = jnp.stack([window_keys.astype(jnp.bfloat16), window_values.astype(jnp.bfloat16)])
    padded = with_halo(stacked, (("nodes", 1),), mesh_rows)
    tile_here = jnp.arange(mesh_tiles, dtype=jnp.int32)[:, None]
    key_rows, value_rows = pick_tiles(
        padded, 3 * mesh_tiles, tile_here + mesh_tiles + window_offsets
    )
    reached = position * mesh_tiles + tile_here + window_offsets
    key_mask = jnp.repeat((reached >= 0) & (reached < all_mesh_tiles), TILE, axis=1)
    windowed = attend_blocks(
        window_queries.reshape(mesh_tiles, TILE, head_columns), key_rows, value_rows, key_mask
    ).reshape(mesh_rows, head_columns)
    (window_terms,) = local_terms(windowed, (gathered[7],))
    window_pieces = lax.all_to_all(
        window_terms.astype(jnp.bfloat16), "heads", split_axis=1, concat_axis=0, tiled=True
    ).astype(window_terms.dtype)
    share_two = (share_one.astype(jnp.float32) + fold_parts(window_pieces, mesh_rows)).astype(
        jnp.bfloat16
    )
    mesh_two = collect(share_two, "heads", 1)
    norm_two = normalize(mesh_two)
    (hidden,) = local_terms(norm_two, (gathered[8],))
    hidden = jax.nn.gelu(hidden, approximate=False).astype(jnp.bfloat16)
    (hidden_terms,) = local_terms(hidden, (gathered[9],))
    hidden_pieces = lax.all_to_all(
        hidden_terms.astype(jnp.bfloat16), "heads", split_axis=1, concat_axis=0, tiled=True
    ).astype(hidden_terms.dtype)
    mesh_out = (share_two.astype(jnp.float32) + fold_parts(hidden_pieces, mesh_rows)).astype(
        jnp.bfloat16
    )
    mesh_three = collect(mesh_out, "heads", 1)
    norm_three = normalize(mesh_three)
    mesh_keys, mesh_values = local_terms(norm_three, (gathered[11], gathered[12]))
    stacked = jnp.stack([mesh_keys.astype(jnp.bfloat16), mesh_values.astype(jnp.bfloat16)])
    padded = with_halo(stacked, (("nodes", 1),), TILE)
    local_index = decoder_blocks - (position * mesh_tiles - 1)
    key_rows, value_rows = pick_tiles(padded, mesh_tiles + 2, local_index)
    key_mask = slot_mask(decoder_count, decoder_blocks.shape[1])
    decoded = attend_blocks(
        grid_queries.reshape(grid_tiles, TILE, head_columns), key_rows, value_rows, key_mask
    ).reshape(grid_rows, head_columns)
    (decoder_terms,) = local_terms(decoded, (gathered[13],))
    decoder_share = sum_at_owner(decoder_terms.astype(jnp.bfloat16), "heads", 1)
    grid_out = (grid_state.astype(jnp.float32) + decoder_share).astype(jnp.bfloat16)
    return (grid_out, mesh_out)


def solution(mesh):
    in_specs = (
        P("nodes", "heads"),
        P("nodes", "heads"),
        P("nodes", "heads"),
        P("nodes", "heads"),
        P("nodes", "heads"),
        P("heads", "nodes"),
        P("nodes", "heads"),
        P("nodes", "heads"),
        P("nodes", "heads"),
        P("heads", "nodes"),
        P("nodes", "heads"),
        P("heads", "nodes"),
        P("nodes", "heads"),
        P("nodes", "heads"),
        P("nodes", "heads"),
        P("heads", "nodes"),
        P("nodes", None),
        P("nodes"),
        P("nodes", None),
        P("nodes", None),
        P("nodes"),
    )
    out_specs = (P("nodes", "heads"), P("nodes", "heads"))
    return jax.shard_map(local, mesh=mesh, in_specs=in_specs, out_specs=out_specs, check_vma=False)
```

profile of v0, /device:TPU:31, one launch (start us, length us, event | category | flops | bytes accessed | tf_op | source)
XLA Modules:
  0.0 417.6 jit_solution(11510416851069582192)
XLA Ops:
  17.6 1.0 copy.55
  19.4 5.6 %all-to-all-start.1 = ((bf16[4,256,256]{1,2,0:T(8,128)(2,1)}), bf16[4,256,256]{1,2,0:T(8,128)(2,1)S(1)}, u32[]{:S(2)}, u32[]{:S(2)}) async-start(bf16[4,256,256]{1,2,0:T(8,128)(2,1)} %broadcast_in_dim.174), calls=%async_computation.1 | async-start | bytes 1048576 | tf_op jit(solution)/shard_map/all_to_all | solution.py:34
  25.2 13.8 %all-to-all-done.1 = bf16[4,256,256]{1,2,0:T(8,128)(2,1)S(1)} async-done(((bf16[4,256,256]{1,2,0:T(8,128)(2,1)}), bf16[4,256,256]{1,2,0:T(8,128)(2,1)S(1)}, u32[]{:S(2)}, u32[]{:S(2)}) %all-to-all-start.1) | async-done | bytes 524320 | tf_op jit(solution)/shard_map/all_to_all | solution.py:34
  39.1 1.6 broadcast_in_dim.168
  40.7 3.7 all-to-all-start
  45.1 53.9 %all-to-all-done = bf16[4,1024,256]{1,2,0:T(8,128)(2,1)S(1)} async-done(((bf16[4,1024,256]{1,2,0:T(8,128)(2,1)}), bf16[4,1024,256]{1,2,0:T(8,128)(2,1)S(1)}, u32[]{:S(2)}, u32[]{:S(2)}) %all-to-all-start) | async-done | bytes 2097184 | tf_op jit(solution)/shard_map/all_to_all | solution.py:34
  100.0 2.0 fusion.8
  102.0 61.1 %all-gather.2.cloned.1.call-done = bf16[1024,2560]{1,0:T(8,128)(2,1)} async-done(((bf16[8,2560]{1,0:T(8,128)(2,1)}), bf16[1024,2560]{1,0:T(8,128)(2,1)}) %all-gather.2.cloned.1.call-update) | async-done | bytes 5242896 | tf_op jit(solution)/shard_map/all_gather | solution.py:16
  163.1 2.4 fusion.14
  165.4 1.7 fusion.13
  167.2 4.0 collective-permute-start
  171.2 1.9 collective-permute-start.1
  173.3 1.3 fusion.15
  174.7 19.8 %collective-permute-done.1 = bf16[2,512,128]{2,1,0:T(8,128)(2,1)S(1)} collective-permute-done((bf16[2,512,128]{2,1,0:T(8,128)(2,1)S(1)}, bf16[2,512,128]{2,1,0:T(8,128)(2,1)S(1)}, u32[]{:S(2)}, u32[]{:S(2)}) %collective-permute-start.1) | collective-permute-done | bytes 262176 | tf_op jit(solution)/shard_map/ppermute | solution.py:49
  194.5 1.0 pad_maximum_fusion
  198.4 1.2 fusion.17
  199.7 1.3 convolution_convert_fusion.4
  201.0 14.9 %all_to_all.69 = bf16[256,4,256]{2,0,1:T(8,128)(2,1)S(1)} all-to-all(bf16[256,4,256]{2,0,1:T(8,128)(2,1)S(1)} %bitcast.190), channel_id=1, replica_groups=mesh['nodes'=128,'heads'=4] {'heads'}, dimensions={1} | all-to-all | bytes 1048576 | tf_op jit(solution)/shard_map/all_to_all | solution.py:203
  217.0 3.5 all-to-all-start.3
  220.7 8.8 %all-to-all-done.3 = bf16[4,256,256]{1,2,0:T(8,128)(2,1)S(1)} async-done(((bf16[4,256,256]{1,2,0:T(8,128)(2,1)}), bf16[4,256,256]{1,2,0:T(8,128)(2,1)S(1)}, u32[]{:S(2)}, u32[]{:S(2)}) %all-to-all-start.3) | async-done | bytes 524320 | tf_op jit(solution)/shard_map/all_to_all | solution.py:34
  230.1 1.3 fusion.19
  231.4 1.3 fusion.18
  232.7 1.9 collective-permute-start.3
  234.6 11.9 %collective-permute-start.2 = (bf16[2,256,128]{2,1,0:T(8,128)(2,1)S(1)}, bf16[2,256,128]{2,1,0:T(8,128)(2,1)S(1)}, u32[]{:S(2)}, u32[]{:S(2)}) collective-permute-start(bf16[2,256,128]{2,1,0:T(8,128)(2,1)S(1)} %pad_maximum_fusion.4), channel_id=1, source_target_pairs={{0,4},{4,8},{8,12},{12,16},{16,20},{20,24},{24,28},{28,32},{32,36}... | collective-permute-start | bytes 393224 | tf_op jit(solution)/shard_map/ppermute | solution.py:48
  246.6 1.3 fusion.16
  248.0 2.9 collective-permute-done.3
  253.3 1.1 fusion.20
  254.5 1.3 convolution_convert_fusion.3
  255.8 17.0 %all_to_all.70 = bf16[256,4,256]{2,0,1:T(8,128)(2,1)S(1)} all-to-all(bf16[256,4,256]{2,0,1:T(8,128)(2,1)S(1)} %bitcast.192), channel_id=1, replica_groups=mesh['nodes'=128,'heads'=4] {'heads'}, dimensions={1} | all-to-all | bytes 1048576 | tf_op jit(solution)/shard_map/all_to_all | solution.py:227
  273.0 12.2 %all_to_all.71 = bf16[4,256,256]{1,2,0:T(8,128)(2,1)S(1)} all-to-all(bf16[4,256,256]{1,2,0:T(8,128)(2,1)S(1)} %broadcast_in_dim.184), channel_id=1, replica_groups=mesh['nodes'=128,'heads'=4] {'heads'}, dimensions={0} | all-to-all | bytes 1048576 | tf_op jit(solution)/shard_map/all_to_all | solution.py:34
  285.8 3.5 convolution_convert_fusion.2
  289.3 14.7 %all_to_all.72 = bf16[256,4,256]{2,0,1:T(8,128)(2,1)S(1)} all-to-all(bf16[256,4,256]{2,0,1:T(8,128)(2,1)S(1)} %bitcast.193), channel_id=1, replica_groups=mesh['nodes'=128,'heads'=4] {'heads'}, dimensions={1} | all-to-all | bytes 1048576 | tf_op jit(solution)/shard_map/all_to_all | solution.py:238
  305.0 4.7 %all-to-all-start.7 = ((bf16[4,256,256]{1,2,0:T(8,128)(2,1)}), bf16[4,256,256]{1,2,0:T(8,128)(2,1)S(1)}, u32[]{:S(2)}, u32[]{:S(2)}) async-start(bf16[4,256,256]{1,2,0:T(8,128)(2,1)} %broadcast_in_dim.185), calls=%async_computation.7 | async-start | bytes 1048576 | tf_op jit(solution)/shard_map/all_to_all | solution.py:34
  310.2 8.7 %all-to-all-done.7 = bf16[4,256,256]{1,2,0:T(8,128)(2,1)S(1)} async-done(((bf16[4,256,256]{1,2,0:T(8,128)(2,1)}), bf16[4,256,256]{1,2,0:T(8,128)(2,1)S(1)}, u32[]{:S(2)}, u32[]{:S(2)}) %all-to-all-start.7) | async-done | bytes 524320 | tf_op jit(solution)/shard_map/all_to_all | solution.py:34
  319.4 1.3 fusion.22
  320.7 1.3 fusion.21
  322.0 17.6 %collective-permute-start.4 = (bf16[2,128,128]{2,1,0:T(8,128)(2,1)S(1)}, bf16[2,128,128]{2,1,0:T(8,128)(2,1)S(1)}, u32[]{:S(2)}, u32[]{:S(2)}) collective-permute-start(bf16[2,128,128]{2,1,0:T(8,128)(2,1)S(1)} %get-tuple-element.121), channel_id=1, source_target_pairs={{0,4},{4,8},{8,12},{12,16},{16,20},{20,24},{24,28},{28,32},{32,36}... | collective-permute-start | bytes 196616 | tf_op jit(solution)/shard_map/ppermute | solution.py:48
  339.6 1.9 collective-permute-start.5
  341.5 1.7 fusion.12
  343.2 12.3 %collective-permute-done.5 = bf16[2,128,128]{2,1,0:T(8,128)(2,1)S(1)} collective-permute-done((bf16[2,128,128]{2,1,0:T(8,128)(2,1)S(1)}, bf16[2,128,128]{2,1,0:T(8,128)(2,1)S(1)}, u32[]{:S(2)}, u32[]{:S(2)}) %collective-permute-start.5) | collective-permute-done | bytes 65568 | tf_op jit(solution)/shard_map/ppermute | solution.py:49
  356.9 12.0 %while.2 = (s32[]{:T(128)}, bf16[2,4,128,128]{3,2,1,0:T(8,128)(2,1)}, bf16[2,4,384,128]{3,2,1,0:T(8,128)(2,1)S(1)}, pred[2,4,384]{2,1,0:T(4,128)(4,1)S(1)}, bf16...) while((s32[]{:T(128)}, bf16[2,4,128,128]{3,2,1,0:T(8,128)(2,1)}, ...), condition=%wide.region_20.21_spmd, body=%wide.region_17.20_spmd.sunk | while | flops 102695296 | bytes 12595925 | solution.py:116
  358.1 1.9 fusion.191
  360.0 2.0 convolution_convert_fusion.14
  364.1 1.9 fusion.191
  366.0 2.0 convolution_convert_fusion.14
  368.9 1.7 convolution_convert_fusion.1
  370.6 38.6 %all_to_all.73 = bf16[4,1024,256]{1,2,0:T(8,128)(2,1)S(1)} all-to-all(bf16[4,1024,256]{1,2,0:T(8,128)(2,1)S(1)} %bitcast.181), channel_id=1, replica_groups=mesh['nodes'=128,'heads'=4] {'heads'}, dimensions={0} | all-to-all | bytes 4194304 | tf_op jit(solution)/shard_map/all_to_all | solution.py:61
  409.8 1.0 copy.75
  (167 shorter events, 29.4 us)
Async XLA Ops:
  7.2 17.9 %copy-start.5 = (bf16[1024,256]{1,0:T(8,128)(2,1)S(1)}, bf16[1024,256]{1,0:T(8,128)(2,1)}, u32[]{:S(2)}) copy-start(bf16[1024,256]{1,0:T(8,128)(2,1)} %param.23) | copy-start | bytes 1572868
  7.2 155.9 %all-gather.2.cloned.1.call-start = ((), (), s32[]{:S(2)}) async-start(), calls=%async_computation.9 | async-start | bytes 5283840 | tf_op jit(solution)/shard_map/all_gather | solution.py:16
  16.9 0.6 copy-start.10
  19.4 19.7 %all-to-all-start.1 = ((bf16[4,256,256]{1,2,0:T(8,128)(2,1)}), bf16[4,256,256]{1,2,0:T(8,128)(2,1)S(1)}, u32[]{:S(2)}, u32[]{:S(2)}) async-start(bf16[4,256,256]{1,2,0:T(8,128)(2,1)} %broadcast_in_dim.174), calls=%async_computation.1 | async-start | bytes 1048576 | tf_op jit(solution)/shard_map/all_to_all | solution.py:34
  40.7 3.8 copy-start.12
  40.7 3.9 copy-start.14
  40.7 58.3 %all-to-all-start = ((bf16[4,1024,256]{1,2,0:T(8,128)(2,1)}), bf16[4,1024,256]{1,2,0:T(8,128)(2,1)S(1)}, u32[]{:S(2)}, u32[]{:S(2)}) async-start(bf16[4,1024,256]{1,2,0:T(8,128)(2,1)} %broadcast_in_dim.168), calls=%async_computation | async-start | bytes 4194304 | tf_op jit(solution)/shard_map/all_to_all | solution.py:34
  102.0 63.5 %copy-start = (bf16[1024,1024]{0,1:T(8,128)(2,1)S(1)}, bf16[1024,1024]{0,1:T(8,128)(2,1)}, u32[]{:S(2)}) copy-start(bf16[1024,1024]{0,1:T(8,128)(2,1)} %fusion.8) | copy-start | bytes 6291460
  167.2 6.1 %copy-start.4 = (bf16[1,1024,128]{2,1,0:T(8,128)(2,1)}, bf16[1,1024,128]{2,1,0:T(8,128)(2,1)S(1)}, u32[]{:S(2)}) copy-start(bf16[1,1024,128]{2,1,0:T(8,128)(2,1)S(1)} %fusion.13) | copy-start | bytes 786436
  167.2 7.4 %collective-permute-start = (bf16[2,512,128]{2,1,0:T(8,128)(2,1)S(1)}, bf16[2,512,128]{2,1,0:T(8,128)(2,1)S(1)}, u32[]{:S(2)}, u32[]{:S(2)}) collective-permute-start(bf16[2,512,128]{2,1,0:T(8,128)(2,1)S(1)} %get-tuple-element.119), channel_id=1, source_target_pairs={{0,4},{4,8},{8,12},{12,16},{16,20},{20,24},{24,28},{28,32},{32,36}... | collective-permute-start | bytes 786440 | tf_op jit(solution)/shard_map/ppermute | solution.py:48
  171.2 23.3 %collective-permute-start.1 = (bf16[2,512,128]{2,1,0:T(8,128)(2,1)S(1)}, bf16[2,512,128]{2,1,0:T(8,128)(2,1)S(1)}, u32[]{:S(2)}, u32[]{:S(2)}) collective-permute-start(bf16[2,512,128]{2,1,0:T(8,128)(2,1)S(1)} %get-tuple-element.120), channel_id=1, source_target_pairs={{4,0},{8,4},{12,8},{16,12},{20,16},{24,20},{28,24},{32,28},{36,32}... | collective-permute-start | bytes 786440 | tf_op jit(solution)/shard_map/ppermute | solution.py:49
  199.6 16.4 %copy-start.6 = (bf16[256,256]{1,0:T(8,128)(2,1)S(1)}, bf16[256,256]{1,0:T(8,128)(2,1)}, u32[]{:S(2)}) copy-start(bf16[256,256]{1,0:T(8,128)(2,1)} %param.24) | copy-start | bytes 393220
  201.0 19.4 %copy-start.13 = (s32[2,4]{1,0:T(2,128)S(1)}, s32[2,4]{1,0:T(2,128)}, u32[]{:S(2)}) copy-start(s32[2,4]{1,0:T(2,128)} %param.41) | copy-start | bytes 100
  217.0 12.6 %all-to-all-start.3 = ((bf16[4,256,256]{1,2,0:T(8,128)(2,1)}), bf16[4,256,256]{1,2,0:T(8,128)(2,1)S(1)}, u32[]{:S(2)}, u32[]{:S(2)}) async-start(bf16[4,256,256]{1,2,0:T(8,128)(2,1)} %broadcast_in_dim.177), calls=%async_computation.3 | async-start | bytes 1048576 | tf_op jit(solution)/shard_map/all_to_all | solution.py:34
  232.7 18.2 %collective-permute-start.3 = (bf16[2,256,128]{2,1,0:T(8,128)(2,1)S(1)}, bf16[2,256,128]{2,1,0:T(8,128)(2,1)S(1)}, u32[]{:S(2)}, u32[]{:S(2)}) collective-permute-start(bf16[2,256,128]{2,1,0:T(8,128)(2,1)S(1)} %pad_maximum_fusion.4), channel_id=1, source_target_pairs={{4,0},{8,4},{12,8},{16,12},{20,16},{24,20},{28,24},{32,28},{36,32}... | collective-permute-start | bytes 393224 | tf_op jit(solution)/shard_map/ppermute | solution.py:49
  234.6 16.2 %collective-permute-start.2 = (bf16[2,256,128]{2,1,0:T(8,128)(2,1)S(1)}, bf16[2,256,128]{2,1,0:T(8,128)(2,1)S(1)}, u32[]{:S(2)}, u32[]{:S(2)}) collective-permute-start(bf16[2,256,128]{2,1,0:T(8,128)(2,1)S(1)} %pad_maximum_fusion.4), channel_id=1, source_target_pairs={{0,4},{4,8},{8,12},{12,16},{16,20},{20,24},{24,28},{28,32},{32,36}... | collective-permute-start | bytes 393224 | tf_op jit(solution)/shard_map/ppermute | solution.py:48
  289.3 20.5 %copy-start.11 = (s32[8,3]{0,1:T(4,128)S(1)}, s32[8,3]{0,1:T(4,128)}, u32[]{:S(2)}) copy-start(s32[8,3]{0,1:T(4,128)} %param.42) | copy-start | bytes 292
  289.3 20.6 %copy-start.15 = (s32[8]{0:T(128)S(1)}, s32[8]{0:T(128)}, u32[]{:S(2)}) copy-start(s32[8]{0:T(128)} %param.43) | copy-start | bytes 100
  304.1 16.6 %copy-start.7 = (bf16[256,256]{1,0:T(8,128)(2,1)}, bf16[256,256]{1,0:T(8,128)(2,1)S(1)}, u32[]{:S(2)}) copy-start(bf16[256,256]{1,0:T(8,128)(2,1)S(1)} %add_convert_fusion.1) | copy-start | bytes 393220
  305.0 13.8 %all-to-all-start.7 = ((bf16[4,256,256]{1,2,0:T(8,128)(2,1)}), bf16[4,256,256]{1,2,0:T(8,128)(2,1)S(1)}, u32[]{:S(2)}, u32[]{:S(2)}) async-start(bf16[4,256,256]{1,2,0:T(8,128)(2,1)} %broadcast_in_dim.185), calls=%async_computation.7 | async-start | bytes 1048576 | tf_op jit(solution)/shard_map/all_to_all | solution.py:34
  309.7 31.8 %copy-start.1 = (bf16[1024,1024]{0,1:T(8,128)(2,1)S(1)}, bf16[1024,1024]{0,1:T(8,128)(2,1)}, u32[]{:S(2)}) copy-start(bf16[1024,1024]{0,1:T(8,128)(2,1)} %fusion.8) | copy-start | bytes 6291460
  322.0 21.2 %collective-permute-start.4 = (bf16[2,128,128]{2,1,0:T(8,128)(2,1)S(1)}, bf16[2,128,128]{2,1,0:T(8,128)(2,1)S(1)}, u32[]{:S(2)}, u32[]{:S(2)}) collective-permute-start(bf16[2,128,128]{2,1,0:T(8,128)(2,1)S(1)} %get-tuple-element.121), channel_id=1, source_target_pairs={{0,4},{4,8},{8,12},{12,16},{16,20},{20,24},{24,28},{28,32},{32,36}... | collective-permute-start | bytes 196616 | tf_op jit(solution)/shard_map/ppermute | solution.py:48
  339.6 16.0 %collective-permute-start.5 = (bf16[2,128,128]{2,1,0:T(8,128)(2,1)S(1)}, bf16[2,128,128]{2,1,0:T(8,128)(2,1)S(1)}, u32[]{:S(2)}, u32[]{:S(2)}) collective-permute-start(bf16[2,128,128]{2,1,0:T(8,128)(2,1)S(1)} %get-tuple-element.122), channel_id=1, source_target_pairs={{4,0},{8,4},{12,8},{16,12},{20,16},{24,20},{28,24},{32,28},{36,32}... | collective-permute-start | bytes 196616 | tf_op jit(solution)/shard_map/ppermute | solution.py:49
  356.9 0.7 copy-start.2
  360.0 2.2 copy-start.8
  360.0 2.9 copy-start.3
  362.2 0.7 copy-start.9
  362.9 0.7 copy-start.2
  366.0 2.2 copy-start.8
  366.0 2.9 copy-start.3
  368.2 0.7 copy-start.9
Sparse Core Ops, SparseCore 0:
  17.7 145.3 all-gather.1
where the time goes:
time: 419 us; the launch traced here: 418 us
  waiting for transfers between devices  181 us (43%)
  blocking collectives  97.4 us (23%)
  starting transfers between devices  56.8 us (14%)
  matrix products  32.7 us (8%)
  local copies, waits for them, and re-layouts  26.6 us (6%)
  between operations  14.7 us (4%)
  other arithmetic  7.87 us (2%)
    all_to_all x4, waiting for transfers between devices, from_everyone(): lax.all_to_all(jnp.broadcast_to(x[None], (length, *x.shape)), axis, 0, 0,...  85.2 us
    all_gather x1, waiting for transfers between devices, turned_gather(): whole = lax.all_gather(both, axis, axis=0, tiled=True)  61.1 us
    all_to_all x1, blocking collectives, sum_at_owner(): lax.all_to_all(parts, axis, split_axis=0, concat_axis=0, tiled=True)  38.6 us
    ppermute x3, waiting for transfers between devices, with_halo(): after = lax.ppermute(first, axis, down)  35 us
    ppermute x3, starting transfers between devices, with_halo(): before = lax.ppermute(last, axis, up)  33.5 us
    dot_general x13, matrix products, local_terms(): jnp.dot(source, member, preferred_element_type=jnp.float32)  21.2 us
    all_to_all x4, starting transfers between devices, from_everyone(): lax.all_to_all(jnp.broadcast_to(x[None], (length, *x.shape)), axis, 0, 0,...  17.5 us
    all_to_all x1, blocking collectives, local(): lax.all_to_all(window_terms.astype(jnp.bfloat16), 'heads', split_axis=1,...  17 us
  transfers between devices with their start and end apart: 11, of which 8 were waited for; matrix products, arithmetic and copies ran while one was open for 3% of the time, Pallas kernels for 0%

commit v1 on v0

--- a/solution.py
+++ b/solution.py
@@ -13,7 +13,14 @@
     turned = [jnp.moveaxis(a, dim, 0) for a, dim in zip(arrays, dims)]
     widths = [t[0].size for t in turned]
     both = jnp.concatenate([t.reshape(-1, w) for t, w in zip(turned, widths)], axis=1)
-    whole = lax.all_gather(both, axis, axis=0, tiled=True)
+
+    def _bind_indices(x0):
+        y_new = jnp.stack([x0 for _ in range(lax.axis_size(axis))], 0)
+        y1 = lax.all_to_all(y_new, axis, 0, 0)
+        heard = jnp.concatenate(y1, 0)
+        return heard
+
+    whole = _bind_indices(both)
     parts = jnp.split(whole, [sum(widths[:k]) for k in range(1, len(widths))], axis=1)
     return tuple(
         (

time: 419 us -> 568 us (1.36)
  the two profiles are of different devices: /device:TPU:31 before, /device:TPU:128 now
where the time goes in v1:
time: 568 us; the launch traced here: 567 us
  waiting for transfers between devices  341 us (60%)
  blocking collectives  112 us (20%)
  starting transfers between devices  54.4 us (10%)
  matrix products  32.9 us (6%)
  local copies, waits for them, and re-layouts  18.6 us (3%)
  other arithmetic  6.85 us (1%)
    all_to_all x1, waiting for transfers between devices, _bind_indices(): y1 = lax.all_to_all(y_new, axis, 0, 0)  226 us
    all_to_all x4, waiting for transfers between devices, from_everyone(): lax.all_to_all(jnp.broadcast_to(x[None], (length, *x.shape)), axis, 0, 0,...  81.2 us
    all_to_all x1, blocking collectives, sum_at_owner(): lax.all_to_all(parts, axis, split_axis=0, concat_axis=0, tiled=True)  41.8 us
    ppermute x3, waiting for transfers between devices, with_halo(): before = lax.ppermute(last, axis, up)  28.6 us
    dot_general x13, matrix products, local_terms(): jnp.dot(source, member, preferred_element_type=jnp.float32)  21.4 us
    all_to_all x1, starting transfers between devices, _bind_indices(): y1 = lax.all_to_all(y_new, axis, 0, 0)  18.7 us
    all_to_all x1, blocking collectives, local(): lax.all_to_all(encoder_terms.astype(jnp.bfloat16), 'heads', split_axis=1,...  18.6 us
    all_to_all x1, blocking collectives, local(): lax.all_to_all(window_terms.astype(jnp.bfloat16), 'heads', split_axis=1,...  17.6 us
  transfers between devices with their start and end apart: 11, of which 10 were waited for; matrix products, arithmetic and copies ran while one was open for 2% of the time, Pallas kernels for 0%

profile of v1, /device:TPU:128, one launch (start us, length us, event | category | flops | bytes accessed | tf_op | source)
XLA Modules:
  0.0 567.0 jit_solution(16983626604767132267)
XLA Ops:
  2.5 5.9 %all-to-all-start.2 = ((bf16[4,256,256]{1,2,0:T(8,128)(2,1)}), bf16[4,256,256]{1,2,0:T(8,128)(2,1)S(1)}, u32[]{:S(2)}, u32[]{:S(2)}) async-start(bf16[4,256,256]{1,2,0:T(8,128)(2,1)} %broadcast_in_dim.174), calls=%async_computation.2 | async-start | bytes 1048576 | tf_op jit(solution)/shard_map/all_to_all | solution.py:41
  8.6 14.3 %all-to-all-done.2 = bf16[4,256,256]{1,2,0:T(8,128)(2,1)S(1)} async-done(((bf16[4,256,256]{1,2,0:T(8,128)(2,1)}), bf16[4,256,256]{1,2,0:T(8,128)(2,1)S(1)}, u32[]{:S(2)}, u32[]{:S(2)}) %all-to-all-start.2) | async-done | bytes 524320 | tf_op jit(solution)/shard_map/all_to_all | solution.py:41
  22.9 1.6 broadcast_in_dim.168
  24.7 3.8 all-to-all-start
  28.7 47.4 %all-to-all-done = bf16[4,1024,256]{1,2,0:T(8,128)(2,1)S(1)} async-done(((bf16[4,1024,256]{1,2,0:T(8,128)(2,1)}), bf16[4,1024,256]{1,2,0:T(8,128)(2,1)S(1)}, u32[]{:S(2)}, u32[]{:S(2)}) %all-to-all-start) | async-done | bytes 2097184 | tf_op jit(solution)/shard_map/all_to_all | solution.py:41
  76.2 2.7 stack.20
  78.8 18.7 %all-to-all-start.1 = ((bf16[128,8,2560]{2,1,0:T(8,128)(2,1)}), bf16[128,8,2560]{2,1,0:T(8,128)(2,1)}, u32[]{:S(2)}, u32[]{:S(2)}) async-start(bf16[128,8,2560]{2,1,0:T(8,128)(2,1)} %stack.20), calls=%async_computation.1 | async-start | bytes 10485760 | tf_op jit(solution)/shard_map/all_to_all | solution.py:19
  99.2 1.9 fusion.8
  101.1 225.8 %all-to-all-done.1 = bf16[128,8,2560]{2,1,0:T(8,128)(2,1)} async-done(((bf16[128,8,2560]{2,1,0:T(8,128)(2,1)}), bf16[128,8,2560]{2,1,0:T(8,128)(2,1)}, u32[]{:S(2)}, u32[]{:S(2)}) %all-to-all-start.1) | async-done | bytes 5242912 | tf_op jit(solution)/shard_map/all_to_all | solution.py:19
  326.9 2.5 fusion.13
  329.4 1.7 fusion.14
  331.2 8.2 %collective-permute-start.1 = (bf16[2,512,128]{2,1,0:T(8,128)(2,1)S(1)}, bf16[2,512,128]{2,1,0:T(8,128)(2,1)S(1)}, u32[]{:S(2)}, u32[]{:S(2)}) collective-permute-start(bf16[2,512,128]{2,1,0:T(8,128)(2,1)S(1)} %get-tuple-element.120), channel_id=1, source_target_pairs={{4,0},{8,4},{12,8},{16,12},{20,16},{24,20},{28,24},{32,28},{36,32}... | collective-permute-start | bytes 786440 | tf_op jit(solution)/shard_map/ppermute | solution.py:56
  339.4 1.9 collective-permute-start
  341.4 1.3 fusion.15
  342.8 3.2 collective-permute-done.1
  346.1 9.2 %collective-permute-done = bf16[2,512,128]{2,1,0:T(8,128)(2,1)S(1)} collective-permute-done((bf16[2,512,128]{2,1,0:T(8,128)(2,1)S(1)}, bf16[2,512,128]{2,1,0:T(8,128)(2,1)S(1)}, u32[]{:S(2)}, u32[]{:S(2)}) %collective-permute-start) | collective-permute-done | bytes 262176 | tf_op jit(solution)/shard_map/ppermute | solution.py:55
  358.3 1.2 fusion.17
  359.6 1.3 convolution_convert_fusion.4
  360.9 18.6 %all_to_all.74 = bf16[256,4,256]{2,0,1:T(8,128)(2,1)S(1)} all-to-all(bf16[256,4,256]{2,0,1:T(8,128)(2,1)S(1)} %bitcast.191), channel_id=1, replica_groups=mesh['nodes'=128,'heads'=4] {'heads'}, dimensions={1} | all-to-all | bytes 1048576 | tf_op jit(solution)/shard_map/all_to_all | solution.py:210
  380.6 3.7 all-to-all-start.4
  384.5 9.8 %all-to-all-done.4 = bf16[4,256,256]{1,2,0:T(8,128)(2,1)S(1)} async-done(((bf16[4,256,256]{1,2,0:T(8,128)(2,1)}), bf16[4,256,256]{1,2,0:T(8,128)(2,1)S(1)}, u32[]{:S(2)}, u32[]{:S(2)}) %all-to-all-start.4) | async-done | bytes 524320 | tf_op jit(solution)/shard_map/all_to_all | solution.py:41
  394.9 1.3 fusion.19
  396.1 1.3 fusion.18
  397.5 1.9 collective-permute-start.3
  399.4 2.4 collective-permute-start.2
  401.8 1.3 fusion.16
  403.2 2.0 collective-permute-done.3
  405.2 10.0 %collective-permute-done.2 = bf16[2,256,128]{2,1,0:T(8,128)(2,1)S(1)} collective-permute-done((bf16[2,256,128]{2,1,0:T(8,128)(2,1)S(1)}, bf16[2,256,128]{2,1,0:T(8,128)(2,1)S(1)}, u32[]{:S(2)}, u32[]{:S(2)}) %collective-permute-start.2) | collective-permute-done | bytes 131104 | tf_op jit(solution)/shard_map/ppermute | solution.py:55
  418.8 1.3 convolution_convert_fusion.3
  420.1 17.6 %all_to_all.75 = bf16[256,4,256]{2,0,1:T(8,128)(2,1)S(1)} all-to-all(bf16[256,4,256]{2,0,1:T(8,128)(2,1)S(1)} %bitcast.193), channel_id=1, replica_groups=mesh['nodes'=128,'heads'=4] {'heads'}, dimensions={1} | all-to-all | bytes 1048576 | tf_op jit(solution)/shard_map/all_to_all | solution.py:234
  438.1 17.4 %all_to_all.76 = bf16[4,256,256]{1,2,0:T(8,128)(2,1)S(1)} all-to-all(bf16[4,256,256]{1,2,0:T(8,128)(2,1)S(1)} %broadcast_in_dim.184), channel_id=1, replica_groups=mesh['nodes'=128,'heads'=4] {'heads'}, dimensions={0} | all-to-all | bytes 1048576 | tf_op jit(solution)/shard_map/all_to_all | solution.py:41
  456.0 3.5 convolution_convert_fusion.2
  459.6 16.2 %all_to_all.77 = bf16[256,4,256]{2,0,1:T(8,128)(2,1)S(1)} all-to-all(bf16[256,4,256]{2,0,1:T(8,128)(2,1)S(1)} %bitcast.194), channel_id=1, replica_groups=mesh['nodes'=128,'heads'=4] {'heads'}, dimensions={1} | all-to-all | bytes 1048576 | tf_op jit(solution)/shard_map/all_to_all | solution.py:245
  476.8 3.5 all-to-all-start.8
  480.8 9.8 %all-to-all-done.8 = bf16[4,256,256]{1,2,0:T(8,128)(2,1)S(1)} async-done(((bf16[4,256,256]{1,2,0:T(8,128)(2,1)}), bf16[4,256,256]{1,2,0:T(8,128)(2,1)S(1)}, u32[]{:S(2)}, u32[]{:S(2)}) %all-to-all-start.8) | async-done | bytes 524320 | tf_op jit(solution)/shard_map/all_to_all | solution.py:41
  491.0 1.3 fusion.21
  492.3 1.3 fusion.22
  493.6 1.9 collective-permute-start.5
  495.6 2.6 collective-permute-start.4
  498.2 1.7 fusion.12
  499.9 9.3 %collective-permute-done.4 = bf16[2,128,128]{2,1,0:T(8,128)(2,1)S(1)} collective-permute-done((bf16[2,128,128]{2,1,0:T(8,128)(2,1)S(1)}, bf16[2,128,128]{2,1,0:T(8,128)(2,1)S(1)}, u32[]{:S(2)}, u32[]{:S(2)}) %collective-permute-start.4) | collective-permute-done | bytes 65568 | tf_op jit(solution)/shard_map/ppermute | solution.py:55
  510.6 11.2 %while.2 = (s32[]{:T(128)}, bf16[2,4,128,128]{3,2,1,0:T(8,128)(2,1)}, bf16[2,4,384,128]{3,2,1,0:T(8,128)(2,1)S(1)}, pred[2,4,384]{2,1,0:T(4,128)(4,1)S(1)}, bf16...) while((s32[]{:T(128)}, bf16[2,4,128,128]{3,2,1,0:T(8,128)(2,1)}, ...), condition=%wide.region_20.21_spmd, body=%wide.region_17.20_spmd.sunk | while | flops 102695296 | bytes 10498717 | solution.py:123
  511.6 1.9 fusion.191
  513.4 2.0 convolution_convert_fusion.14
  517.2 1.9 fusion.191
  519.0 2.0 convolution_convert_fusion.14
  521.9 1.7 convolution_convert_fusion.1
  523.6 41.8 %all_to_all.78 = bf16[4,1024,256]{1,2,0:T(8,128)(2,1)S(1)} all-to-all(bf16[4,1024,256]{1,2,0:T(8,128)(2,1)S(1)} %bitcast.182), channel_id=1, replica_groups=mesh['nodes'=128,'heads'=4] {'heads'}, dimensions={0} | all-to-all | bytes 4194304 | tf_op jit(solution)/shard_map/all_to_all | solution.py:68
  (183 shorter events, 21.8 us)
Async XLA Ops:
  0.6 7.8 %copy-start.4 = (bf16[1024,256]{1,0:T(8,128)(2,1)S(1)}, bf16[1024,256]{1,0:T(8,128)(2,1)}, u32[]{:S(2)}) copy-start(bf16[1024,256]{1,0:T(8,128)(2,1)} %param.23) | copy-start | bytes 1572868
  2.5 20.4 %all-to-all-start.2 = ((bf16[4,256,256]{1,2,0:T(8,128)(2,1)}), bf16[4,256,256]{1,2,0:T(8,128)(2,1)S(1)}, u32[]{:S(2)}, u32[]{:S(2)}) async-start(bf16[4,256,256]{1,2,0:T(8,128)(2,1)} %broadcast_in_dim.174), calls=%async_computation.2 | async-start | bytes 1048576 | tf_op jit(solution)/shard_map/all_to_all | solution.py:41
  24.5 3.9 copy-start.9
  24.5 3.9 copy-start.10
  24.5 3.9 copy-start.11
  24.5 4.0 copy-start.12
  24.6 4.0 copy-start.13
  24.6 4.0 copy-start.14
  24.6 4.0 copy-start.15
  24.6 4.0 copy-start.16
  24.6 4.0 copy-start.7
  24.6 4.0 copy-start.8
  24.6 4.0 copy-start.17
  24.6 4.0 copy-start.18
  24.6 4.0 copy-start.19
  24.7 4.1 copy-start.20
  24.7 51.5 %all-to-all-start = ((bf16[4,1024,256]{1,2,0:T(8,128)(2,1)}), bf16[4,1024,256]{1,2,0:T(8,128)(2,1)S(1)}, u32[]{:S(2)}, u32[]{:S(2)}) async-start(bf16[4,1024,256]{1,2,0:T(8,128)(2,1)} %broadcast_in_dim.168), calls=%async_computation | async-start | bytes 4194304 | tf_op jit(solution)/shard_map/all_to_all | solution.py:41
  78.8 18.7 %copy-start.22 = (s32[2,8]{1,0:T(2,128)S(1)}, s32[2,8]{1,0:T(2,128)}, u32[]{:S(2)}) copy-start(s32[2,8]{1,0:T(2,128)} %param.39) | copy-start | bytes 196
  78.8 18.8 %copy-start.24 = (s32[2]{0:T(128)S(1)}, s32[2]{0:T(128)}, u32[]{:S(2)}) copy-start(s32[2]{0:T(128)} %param.40) | copy-start | bytes 28
  78.8 248.1 %all-to-all-start.1 = ((bf16[128,8,2560]{2,1,0:T(8,128)(2,1)}), bf16[128,8,2560]{2,1,0:T(8,128)(2,1)}, u32[]{:S(2)}, u32[]{:S(2)}) async-start(bf16[128,8,2560]{2,1,0:T(8,128)(2,1)} %stack.20), calls=%async_computation.1 | async-start | bytes 10485760 | tf_op jit(solution)/shard_map/all_to_all | solution.py:19
  326.9 2.5 copy-start
  331.2 14.9 %collective-permute-start.1 = (bf16[2,512,128]{2,1,0:T(8,128)(2,1)S(1)}, bf16[2,512,128]{2,1,0:T(8,128)(2,1)S(1)}, u32[]{:S(2)}, u32[]{:S(2)}) collective-permute-start(bf16[2,512,128]{2,1,0:T(8,128)(2,1)S(1)} %get-tuple-element.120), channel_id=1, source_target_pairs={{4,0},{8,4},{12,8},{16,12},{20,16},{24,20},{28,24},{32,28},{36,32}... | collective-permute-start | bytes 786440 | tf_op jit(solution)/shard_map/ppermute | solution.py:56
  339.4 15.9 %collective-permute-start = (bf16[2,512,128]{2,1,0:T(8,128)(2,1)S(1)}, bf16[2,512,128]{2,1,0:T(8,128)(2,1)S(1)}, u32[]{:S(2)}, u32[]{:S(2)}) collective-permute-start(bf16[2,512,128]{2,1,0:T(8,128)(2,1)S(1)} %get-tuple-element.119), channel_id=1, source_target_pairs={{0,4},{4,8},{8,12},{12,16},{16,20},{20,24},{24,28},{28,32},{32,36}... | collective-permute-start | bytes 786440 | tf_op jit(solution)/shard_map/ppermute | solution.py:55
  359.5 20.1 %copy-start.5 = (bf16[256,256]{1,0:T(8,128)(2,1)S(1)}, bf16[256,256]{1,0:T(8,128)(2,1)}, u32[]{:S(2)}) copy-start(bf16[256,256]{1,0:T(8,128)(2,1)} %param.24) | copy-start | bytes 393220
  360.9 23.4 %copy-start.23 = (s32[2,4]{1,0:T(2,128)S(1)}, s32[2,4]{1,0:T(2,128)}, u32[]{:S(2)}) copy-start(s32[2,4]{1,0:T(2,128)} %param.41) | copy-start | bytes 100
  380.6 13.7 %all-to-all-start.4 = ((bf16[4,256,256]{1,2,0:T(8,128)(2,1)}), bf16[4,256,256]{1,2,0:T(8,128)(2,1)S(1)}, u32[]{:S(2)}, u32[]{:S(2)}) async-start(bf16[4,256,256]{1,2,0:T(8,128)(2,1)} %broadcast_in_dim.177), calls=%async_computation.4 | async-start | bytes 1048576 | tf_op jit(solution)/shard_map/all_to_all | solution.py:41
  397.5 7.7 %collective-permute-start.3 = (bf16[2,256,128]{2,1,0:T(8,128)(2,1)S(1)}, bf16[2,256,128]{2,1,0:T(8,128)(2,1)S(1)}, u32[]{:S(2)}, u32[]{:S(2)}) collective-permute-start(bf16[2,256,128]{2,1,0:T(8,128)(2,1)S(1)} %pad_maximum_fusion.4), channel_id=1, source_target_pairs={{4,0},{8,4},{12,8},{16,12},{20,16},{24,20},{28,24},{32,28},{36,32}... | collective-permute-start | bytes 393224 | tf_op jit(solution)/shard_map/ppermute | solution.py:56
  399.4 15.8 %collective-permute-start.2 = (bf16[2,256,128]{2,1,0:T(8,128)(2,1)S(1)}, bf16[2,256,128]{2,1,0:T(8,128)(2,1)S(1)}, u32[]{:S(2)}, u32[]{:S(2)}) collective-permute-start(bf16[2,256,128]{2,1,0:T(8,128)(2,1)S(1)} %pad_maximum_fusion.4), channel_id=1, source_target_pairs={{0,4},{4,8},{8,12},{12,16},{16,20},{20,24},{24,28},{28,32},{32,36}... | collective-permute-start | bytes 393224 | tf_op jit(solution)/shard_map/ppermute | solution.py:55
  459.5 20.8 %copy-start.21 = (s32[8,3]{0,1:T(4,128)S(1)}, s32[8,3]{0,1:T(4,128)}, u32[]{:S(2)}) copy-start(s32[8,3]{0,1:T(4,128)} %param.42) | copy-start | bytes 292
  459.6 21.0 %copy-start.25 = (s32[8]{0:T(128)S(1)}, s32[8]{0:T(128)}, u32[]{:S(2)}) copy-start(s32[8]{0:T(128)} %param.43) | copy-start | bytes 100
  475.9 0.9 copy-start.6
  476.8 13.7 %all-to-all-start.8 = ((bf16[4,256,256]{1,2,0:T(8,128)(2,1)}), bf16[4,256,256]{1,2,0:T(8,128)(2,1)S(1)}, u32[]{:S(2)}, u32[]{:S(2)}) async-start(bf16[4,256,256]{1,2,0:T(8,128)(2,1)} %broadcast_in_dim.185), calls=%async_computation.8 | async-start | bytes 1048576 | tf_op jit(solution)/shard_map/all_to_all | solution.py:41
  480.3 17.9 %copy-start.1 = (bf16[1024,1024]{0,1:T(8,128)(2,1)S(1)}, bf16[1024,1024]{0,1:T(8,128)(2,1)}, u32[]{:S(2)}) copy-start(bf16[1024,1024]{0,1:T(8,128)(2,1)} %fusion.8) | copy-start | bytes 6291460
  493.6 6.3 %collective-permute-start.5 = (bf16[2,128,128]{2,1,0:T(8,128)(2,1)S(1)}, bf16[2,128,128]{2,1,0:T(8,128)(2,1)S(1)}, u32[]{:S(2)}, u32[]{:S(2)}) collective-permute-start(bf16[2,128,128]{2,1,0:T(8,128)(2,1)S(1)} %get-tuple-element.122), channel_id=1, source_target_pairs={{4,0},{8,4},{12,8},{16,12},{20,16},{24,20},{28,24},{32,28},{36,32}... | collective-permute-start | bytes 196616 | tf_op jit(solution)/shard_map/ppermute | solution.py:56
  495.6 13.7 %collective-permute-start.4 = (bf16[2,128,128]{2,1,0:T(8,128)(2,1)S(1)}, bf16[2,128,128]{2,1,0:T(8,128)(2,1)S(1)}, u32[]{:S(2)}, u32[]{:S(2)}) collective-permute-start(bf16[2,128,128]{2,1,0:T(8,128)(2,1)S(1)} %get-tuple-element.121), channel_id=1, source_target_pairs={{0,4},{4,8},{8,12},{12,16},{16,20},{20,24},{24,28},{28,32},{32,36}... | collective-permute-start | bytes 196616 | tf_op jit(solution)/shard_map/ppermute | solution.py:55
  510.6 0.7 copy-start.2
  513.4 2.8 copy-start.3
  516.2 0.7 copy-start.2
  519.0 2.8 copy-start.3
